TPU v7x, 32 devices: a whole 2x2x4 slice. The times are simulated.
32 devices in a mesh: gx: 2 (over x), gy: 4 (over y, core), gz: 4 (over z).
Axes of the slice: x: 2, y: 2, z: 4, core: 2. Of those that a mesh axis runs over, the one named last changes fastest.
Arguments:
- density: float32 [10, 20, 640], P('gx', 'gy', 'gz'), may hold values from 0.5 to 2
- velocity: float32 [3, 10, 20, 640], P(None, 'gx', 'gy', 'gz'), may hold values from -3.2 to 3.2
- pressure: float32 [10, 20, 640], P('gx', 'gy', 'gz'), may hold values from 0.5 to 2
- blending: float32 [2, 4, 128], P('gx', 'gy', 'gz'), may hold values from 0 to 0.6
- face_signal_weights: bfloat16 [4, 1280, 4096], P(None, ('gx', 'gy'), 'gz'), may hold values from -0.03125 to 0.03125
- surf_id: int32 [3840], P(('gx', 'gy', 'gz')), may hold values from -1 to 1279, as said below
- surface_face_code: int32 [3840], P(('gx', 'gy', 'gz')), may hold values from 0 to 191, as said below
Outputs:
- tendency: float32 [5, 10, 20, 640], P(None, 'gx', 'gy', 'gz')
- signals: float32 [4096], P(('gz', 'gx', 'gy'))
Inputs may be any that keep to these rules, and one draw needn't show every extreme that they name: `surf_id`: every face id 0 to 1279 stands in exactly one slot; a device's listed faces fill its first slots and its other slots hold -1. A quarter of the devices list exactly 120 faces, the others at most 40. `surface_face_code`: the codes of one device are distinct.
All inputs are finite; a program needn't handle non-finite values.
Results may differ from a plain program's by a relative error of at most 0.0029.
Values may be sent and summed in bfloat16 or wider, within the bound.
A program may use at most 128 MiB of HBM per device.

v0:
```python
import functools
import math

import jax
import jax.numpy as jnp
import numpy as np
from jax import lax
from jax.experimental import pallas as pl
from jax.experimental.pallas import tpu as pltpu
from jax.sharding import PartitionSpec as P

GAMMA = 1.4
MESH = pl.DeviceIdType.MESH
F32 = jnp.float32
BF16 = jnp.bfloat16


def gauss_lobatto():
    inner_root = math.sqrt(3.0 / 7.0)
    points = np.array([-1.0, -inner_root, 0.0, inner_root, 1.0])
    quad_weights = np.array([0.1, 49.0 / 90.0, 32.0 / 45.0, 49.0 / 90.0, 0.1])
    barycentric = np.ones(5)
    for target in range(5):
        for source in range(5):
            if source != target:
                barycentric[target] = barycentric[target] / (points[target] - points[source])
    derivative = np.zeros((5, 5))
    for target in range(5):
        for source in range(5):
            if source != target:
                derivative[target, source] = (
                    barycentric[source] / barycentric[target] / (points[target] - points[source])
                )
        derivative[target, target] = -np.sum(derivative[target])
    return (derivative, quad_weights)


DERIV, QUAD = gauss_lobatto()
NODES = len(QUAD)


def up(value, step):
    return (value + step - 1) // step * step


def pick(index, table):
    out = jnp.zeros(index.shape, F32)
    for key, value in table.items():
        out = jnp.where(index == key, F32(value), out)
    return out


def with_energy(prim):
    rho, u, v, w, p = prim
    specific = p / rho * (1.0 / (GAMMA - 1.0)) + 0.5 * (u * u + v * v + w * w)
    return (rho, u, v, w, specific, p)


def pair_flux(a, b, d):
    r, s1, s2, s3, se, sp = (x + y for x, y in zip(a, b))
    speeds = (s1, s2, s3)
    m = r * speeds[d]
    parts = [m + m]
    for c in range(3):
        parts.append(m * speeds[c] + 4.0 * sp if c == d else m * speeds[c])
    parts.append(m * se + 2.0 * (sp * speeds[d]))
    return parts


def node_state(a, d):
    rho, u, v, w, specific, p = a
    speeds = (u, v, w)
    energy = rho * specific
    cons = [rho, rho * u, rho * v, rho * w, energy]
    normal = speeds[d]
    flux = [cons[1 + d]]
    for c in range(3):
        part = cons[1 + c] * normal
        flux.append(part + p if c == d else part)
    flux.append((energy + p) * normal)
    return flux, cons, jnp.abs(normal) + jnp.sqrt(GAMMA * (p / rho))


def rusanov2(left, right):
    (fl, ul, sl), (fr, ur, sr) = left, right
    fastest = jnp.maximum(sl, sr)
    return [a + b - fastest * (d - c) for a, b, c, d in zip(fl, fr, ul, ur)]


def kernel(
    sizes,
    den_h, vel_h, pre_h, ble_h, wei_h, id_h, code_h,
    tend_ref, sig_ref,
    den, vel, pre, ble, wei, ids, codes,
    prim, acc, coef, ystage, yghost, zstage, zghost,
    mine, faces_in, part, parts_in, stage, sums_in,
    in_sem, halo_send, halo_recv, face_send, face_recv, z_send, z_recv, rs_send, rs_recv,
):
    nx_dev, ny_dev, nz_dev = sizes
    groups = nx_dev * ny_dev
    px, py, pz = den_h.shape
    elems = ble_h.shape[-1]
    slots = id_h.shape[-1]
    lanes = prim.shape[-1]
    rows = prim.shape[-2]
    quantities, shard_faces, local_signals = wei_h.shape
    own = local_signals // groups

    gx, gy, gz = lax.axis_index("gx"), lax.axis_index("gy"), lax.axis_index("gz")
    group = gx * ny_dev + gy

    def in_group(step):
        other = lax.rem(group + step, groups)
        return (lax.div(other, ny_dev), lax.rem(other, ny_dev), gz)

    def in_column(step):
        return (gx, gy, lax.rem(gz + step, nz_dev))

    barrier = pltpu.get_barrier_semaphore()
    for step in range(1, groups):
        pl.semaphore_signal(barrier, inc=1, device_id=in_group(step), device_id_type=MESH)
    for step in range(1, nz_dev):
        pl.semaphore_signal(barrier, inc=1, device_id=in_column(step), device_id_type=MESH)

    loads = [
        pltpu.make_async_copy(src, dst, in_sem.at[n])
        for n, (src, dst) in enumerate(
            ((den_h, den), (vel_h, vel), (pre_h, pre), (ble_h, ble), (id_h, ids), (code_h, codes), (wei_h, wei))
        )
    ]
    for load in loads:
        load.start()

    row = lax.broadcasted_iota(jnp.int32, (rows, lanes), 0)
    lane = lax.broadcasted_iota(jnp.int32, (rows, lanes), 1)
    lane_node = lax.rem(lane, NODES)
    row_weight = pick(row, {i: QUAD[i] for i in range(NODES)})

    width = up(3 * elems, 128)
    z_at = lax.broadcasted_iota(jnp.int32, (lanes, width), 0)
    c_at = lax.broadcasted_iota(jnp.int32, (lanes, width), 1)
    element = lax.div(z_at, NODES)
    node = z_at - NODES * element
    reduce_z = jnp.where(element == c_at, pick(node, {i: QUAD[i] for i in range(NODES)}), F32(0))
    reduce_z = jnp.where((element + elems == c_at) & (node == 0), F32(-1), reduce_z)
    reduce_z = jnp.where((element + 2 * elems == c_at) & (node == NODES - 1), F32(1), reduce_z)
    reduce_z = jnp.where(z_at < pz, reduce_z, F32(0))

    prim[:, 0:px] = jnp.ones((5, px, rows, lanes), F32)
    for n in range(3):
        loads[n].wait()
    for x in range(px):
        prim[0, x, 0:py, 0:pz] = den[x]
        for c in range(3):
            prim[1 + c, x, 0:py, 0:pz] = vel[c, x]
        prim[4, x, 0:py, 0:pz] = pre[x]

    def mass_momentum(x, d):
        rho, u, v, w, p = (prim[f, x] for f in range(5))
        speeds = (u, v, w)
        m = rho * speeds[d]
        return [m] + [m * speeds[c] + p if c == d else m * speeds[c] for c in range(3)]

    def rows_of(values, sign):
        out = jnp.zeros((rows, lanes), F32)
        for q in range(quantities):
            out = jnp.where(row == q, sign * values[q], out)
        return out

    tables = []
    for x, sign in ((0, -1.0), (px - 1, 1.0)):
        sums = [jnp.sum(row_weight * f, axis=0, keepdims=True) for f in mass_momentum(x, 0)]
        tables.append(rows_of(sums, sign))
    along_y = [jnp.zeros((rows, lanes), F32)] * quantities
    along_z = [jnp.zeros((rows, lanes), F32)] * quantities
    for x in range(px):
        along_y = [a + F32(QUAD[x]) * f for a, f in zip(along_y, mass_momentum(x, 1))]
        along_z = [a + F32(QUAD[x]) * f for a, f in zip(along_z, mass_momentum(x, 2))]
    for y, sign in ((0, -1.0), (py - 1, 1.0)):
        tables.append(rows_of([a[y : y + 1] for a in along_y], sign))
    tables.append(rows_of([jnp.sum(row_weight * a, axis=0, keepdims=True) for a in along_z], 1.0))
    table = jnp.dot(
        jnp.concatenate(tables, axis=0), reduce_z,
        precision=lax.Precision.HIGHEST, preferred_element_type=F32,
    ).astype(BF16)

    for n in range(3, 6):
        loads[n].wait()
    pad = mine.shape[-1]
    code_row = jnp.concatenate([codes[...], jnp.full((1, pad - slots), -1, jnp.int32)], axis=1) if pad > slots else codes[...]
    id_row = jnp.concatenate([ids[...], jnp.full((1, pad - slots), -1, jnp.int32)], axis=1) if pad > slots else ids[...]
    r_at = lax.broadcasted_iota(jnp.int32, (width, pad), 0)
    chosen = []
    for f in range(4):
        hit = (code_row == r_at + f * elems) & (r_at < elems)
        chosen.append(jnp.where(hit, F32(1), F32(0)).astype(BF16))
    hit = (code_row == r_at + 3 * elems) & (r_at >= elems) & (r_at < 3 * elems)
    chosen.append(jnp.where(hit, F32(1), F32(0)).astype(BF16))
    face_values = jnp.dot(
        jnp.concatenate([table[rows * f : rows * f + rows] for f in range(5)], axis=1),
        jnp.concatenate(chosen, axis=0),
        preferred_element_type=F32,
    )
    slot_row = lax.broadcasted_iota(jnp.int32, (rows, pad), 0)
    mine[...] = jnp.where(slot_row == quantities, id_row.astype(F32), face_values)

    ystage[...] = jnp.ones(ystage.shape, F32)
    for x in range(px):
        for f in range(5):
            ystage[0, f, x : x + 1, :] = prim[f, x, 0:1, :]
            ystage[1, f, x : x + 1, :] = prim[f, x, py - 1 : py, :]
    zlane = lax.broadcasted_iota(jnp.int32, (rows, 128), 1)
    for side, at in ((0, 0), (1, pz - 1)):
        packed = jnp.ones((rows, 128), F32)
        for f in range(5):
            for x in range(px):
                packed = jnp.where(zlane == f * px + x, prim[f, x, :, at : at + 1], packed)
        zstage[side] = packed

    pl.semaphore_wait(barrier, groups - 1 + nz_dev - 1)

    def remote(src, dst, send, recv, device):
        return pltpu.make_async_remote_copy(
            src_ref=src, dst_ref=dst, send_sem=send, recv_sem=recv, device_id=device, device_id_type=MESH
        )

    face_copies = [
        remote(mine, faces_in.at[k - 1], face_send.at[k - 1], face_recv.at[k - 1], in_group(k))
        for k in range(1, groups)
    ]
    for copy in face_copies:
        copy.start()

    def beside(axis, step):
        at = [gx, gy, gz]
        at[axis] = lax.rem(at[axis] + sizes[axis] + step, sizes[axis])
        return tuple(at)

    halo_copies = [
        remote(prim.at[:, px - 1], prim.at[:, px + 1], halo_send.at[0], halo_recv.at[0], beside(0, 1)),
        remote(prim.at[:, 0], prim.at[:, px], halo_send.at[1], halo_recv.at[1], beside(0, -1)),
        remote(ystage.at[1], yghost.at[0], halo_send.at[2], halo_recv.at[2], beside(1, 1)),
        remote(ystage.at[0], yghost.at[1], halo_send.at[3], halo_recv.at[3], beside(1, -1)),
        remote(zstage.at[1], zghost.at[0], halo_send.at[4], halo_recv.at[4], beside(2, 1)),
        remote(zstage.at[0], zghost.at[1], halo_send.at[5], halo_recv.at[5], beside(2, -1)),
    ]
    for copy in halo_copies:
        copy.start()

    spread_e = lax.broadcasted_iota(jnp.int32, (elems, lanes), 0)
    spread_z = lax.broadcasted_iota(jnp.int32, (elems, lanes), 1)
    spread = jnp.where(lax.div(spread_z, NODES) == spread_e, F32(1), F32(0))
    alpha = jnp.dot(
        jnp.broadcast_to(ble[0], (rows, elems)), spread,
        precision=lax.Precision.HIGHEST, preferred_element_type=F32,
    )
    volume = jnp.where(lane < pz, (alpha - 1.0) * 0.25, F32(0))
    for d, at in ((0, row), (1, lane_node)):
        for k in range(1, NODES):
            base = 8 * d + 2 * (k - 1)
            coef[base] = volume * pick(at, {i: DERIV[i, i + k] for i in range(NODES - k)})
            coef[base + 1] = volume * pick(at, {i: DERIV[i + k, i] for i in range(NODES - k)})
        half = pick(at, {i: 0.5 / QUAD[i] for i in range(NODES)})
        coef[16 + 2 * d] = -half * jnp.where(at == NODES - 1, F32(1), alpha)
        coef[17 + 2 * d] = half * jnp.where(at == 0, F32(1), alpha)
    coef[20] = volume
    coef[21] = alpha

    def plane(x):
        return with_energy(tuple(prim[f, x] for f in range(5)))

    def inside(x, carry):
        here = plane(x)
        total = [acc[q, x] for q in range(5)]
        for d, axis, size in ((1, 0, rows), (2, 1, lanes)):
            for k in range(1, NODES):
                there = tuple(pltpu.roll(a, size - k, axis) for a in here)
                flux = pair_flux(here, there, d)
                base = 8 * (d - 1) + 2 * (k - 1)
                forward, back = coef[base], coef[base + 1]
                total = [t + forward * f + pltpu.roll(back * f, k, axis) for t, f in zip(total, flux)]
        for q in range(5):
            acc[q, x] = total[q]
        return carry

    planes = [plane(x) for x in range(px)]
    for x in range(px):
        total = [jnp.zeros((rows, lanes), F32)] * 5
        for other in range(px):
            if other != x:
                flux = pair_flux(planes[x], planes[other], 0)
                total = [t + F32(DERIV[x, other]) * f for t, f in zip(total, flux)]
        for q in range(5):
            acc[q, x] = coef[20] * total[q]
    lax.fori_loop(0, px, inside, 0, unroll=True)

    for copy in face_copies:
        copy.wait()
    wanted = lax.broadcasted_iota(jnp.int32, (shard_faces, pad), 0).astype(F32)
    start = (group * shard_faces).astype(F32)
    arrived = [mine[...]] + [faces_in[k] for k in range(groups - 1)]
    placing = [
        jnp.where(a[quantities : quantities + 1] - start == wanted, F32(1), F32(0)).astype(BF16) for a in arrived
    ]
    part[...] = lax.dot_general(
        jnp.concatenate([a.astype(BF16) for a in arrived], axis=1),
        jnp.concatenate(placing, axis=1),
        (((1,), (1,)), ((), ())),
        preferred_element_type=F32,
    )
    z_copies = [
        remote(part, parts_in.at[k - 1], z_send.at[k - 1], z_recv.at[k - 1], in_column(k))
        for k in range(1, nz_dev)
    ]
    for copy in z_copies:
        copy.start()

    for copy in halo_copies:
        copy.wait()
    low, high = zghost[0], zghost[1]
    for f in range(5):
        for x in range(px):
            prim[f, x, py : py + 1, :] = yghost[1, f, x : x + 1, :]
            prim[f, x, rows - 1 : rows, :] = yghost[0, f, x : x + 1, :]
            at = f * px + x
            first = pz // 128 * 128
            block = prim[f, x, :, first : first + 128]
            block = jnp.where(zlane == pz - first, high[:, at : at + 1], block)
            if first + 128 == lanes:
                block = jnp.where(zlane == 127, low[:, at : at + 1], block)
            else:
                last = prim[f, x, :, lanes - 128 : lanes]
                prim[f, x, :, lanes - 128 : lanes] = jnp.where(zlane == 127, low[:, at : at + 1], last)
            prim[f, x, :, first : first + 128] = block

    def between(x, carry):
        here = plane(x)
        total = [acc[q, x] for q in range(5)]
        for d, axis, size in ((1, 0, rows), (2, 1, lanes)):
            state = node_state(here, d)
            after = (
                [pltpu.roll(a, size - 1, axis) for a in state[0]],
                [pltpu.roll(a, size - 1, axis) for a in state[1]],
                pltpu.roll(state[2], size - 1, axis),
            )
            upper, lower = coef[14 + 2 * d], coef[15 + 2 * d]
            edge = rusanov2(state, after)
            total = [t + upper * e + lower * pltpu.roll(e, 1, axis) for t, e in zip(total, edge)]
        for q in range(5):
            acc[q, x] = total[q]
        return carry

    lax.fori_loop(0, px, between, 0, unroll=True)

    before = node_state(plane(px + 1), 0)
    current = node_state(plane(0), 0)
    below = rusanov2(before, current)
    for x in range(px):
        following = node_state(plane(x + 1), 0)
        above = rusanov2(current, following)
        half = F32(0.5 / QUAD[x])
        for q in range(5):
            out = acc[q, x]
            mix = coef[21] * half
            out = out - (half if x == px - 1 else mix) * above[q]
            out = out + (half if x == 0 else mix) * below[q]
            tend_ref[q, x] = out[0:py, 0:pz]
        current, below = following, above

    for copy in z_copies:
        copy.wait()
    loads[6].wait()
    data = part[...]
    for k in range(nz_dev - 1):
        data = data + parts_in[k]
    data = data.astype(BF16)
    data_row = lax.broadcasted_iota(jnp.int32, data.shape, 0)
    result = jnp.zeros((rows, local_signals), F32)
    for q in range(quantities):
        result = result + jnp.dot(
            jnp.where(data_row == q, data, jnp.zeros((), BF16)), wei[q], preferred_element_type=F32
        )
    result = jnp.sum(result, axis=0, keepdims=True)
    for t in range(groups):
        stage[t] = result[:, t * own : (t + 1) * own]
    rs_copies = []
    for k in range(1, groups):
        other = lax.rem(group + k, groups)
        rs_copies.append(
            remote(stage.at[other], sums_in.at[k - 1], rs_send.at[k - 1], rs_recv.at[k - 1], in_group(k))
        )
    for copy in rs_copies:
        copy.start()
    for copy in rs_copies:
        copy.wait()
    total = stage[group]
    for k in range(groups - 1):
        total = total + sums_in[k]
    sig_ref[...] = total


def shards(sizes, density, velocity, pressure, blending, face_signal_weights, surf_id, surface_face_code):
    groups = sizes[0] * sizes[1]
    px, py, pz = density.shape
    assert blending.shape[:2] == (1, 1) and px == NODES and py == NODES
    rows, lanes = up(py + 2, 8), up(pz + 2, 128)
    slots = surf_id.shape[0]
    pad = up(slots, 128)
    quantities, shard_faces, local_signals = face_signal_weights.shape
    own = local_signals // groups
    dma = pltpu.SemaphoreType.DMA
    tendency, signals = pl.pallas_call(
        functools.partial(kernel, sizes),
        out_shape=(
            jax.ShapeDtypeStruct((5, px, py, pz), F32),
            jax.ShapeDtypeStruct((1, own), F32),
        ),
        in_specs=[pl.BlockSpec(memory_space=pl.ANY)] * 7,
        out_specs=(pl.BlockSpec(memory_space=pltpu.VMEM), pl.BlockSpec(memory_space=pltpu.VMEM)),
        scratch_shapes=[
            pltpu.VMEM(density.shape, F32),
            pltpu.VMEM(velocity.shape, F32),
            pltpu.VMEM(pressure.shape, F32),
            pltpu.VMEM(blending.shape, F32),
            pltpu.VMEM(face_signal_weights.shape, BF16),
            pltpu.VMEM((1, slots), jnp.int32),
            pltpu.VMEM((1, slots), jnp.int32),
            pltpu.VMEM((5, px + 2, rows, lanes), F32),
            pltpu.VMEM((5, px, rows, lanes), F32),
            pltpu.VMEM((22, rows, lanes), F32),
            pltpu.VMEM((2, 5, rows, lanes), F32),
            pltpu.VMEM((2, 5, rows, lanes), F32),
            pltpu.VMEM((2, rows, 128), F32),
            pltpu.VMEM((2, rows, 128), F32),
            pltpu.VMEM((rows, pad), F32),
            pltpu.VMEM((groups - 1, rows, pad), F32),
            pltpu.VMEM((rows, shard_faces), F32),
            pltpu.VMEM((sizes[2] - 1, rows, shard_faces), F32),
            pltpu.VMEM((groups, 1, own), F32),
            pltpu.VMEM((groups - 1, 1, own), F32),
            dma((7,)),
            dma((6,)),
            dma((6,)),
            dma((groups - 1,)),
            dma((groups - 1,)),
            dma((sizes[2] - 1,)),
            dma((sizes[2] - 1,)),
            dma((groups - 1,)),
            dma((groups - 1,)),
        ],
        compiler_params=pltpu.CompilerParams(collective_id=0, has_side_effects=True),
    )(
        density, velocity, pressure, blending, face_signal_weights,
        surf_id.reshape(1, -1), surface_face_code.reshape(1, -1),
    )
    return tendency, signals.reshape(-1)


def solution(mesh):
    sizes = (mesh.shape["gx"], mesh.shape["gy"], mesh.shape["gz"])
    placed = (
        P("gx", "gy", "gz"),
        P(None, "gx", "gy", "gz"),
        P("gx", "gy", "gz"),
        P("gx", "gy", "gz"),
        P(None, ("gx", "gy"), "gz"),
        P(("gx", "gy", "gz")),
        P(("gx", "gy", "gz")),
    )
    return jax.shard_map(
        functools.partial(shards, sizes),
        mesh=mesh,
        in_specs=placed,
        out_specs=(P(None, "gx", "gy", "gz"), P(("gz", "gx", "gy"))),
        check_vma=False,
    )
```

profile of v0, /device:TPU:0, one launch (start us, length us, event | category | flops | bytes accessed | tf_op | source)
XLA Modules:
  0.0 22.3 jit_solution(8074761595579678142)
XLA Ops:
  0.6 1.6 %copy.9.vel_h = f32[3,5,5,160]{3,2,1,0:T(8,128)} copy(f32[3,5,5,160]{3,0,2,1:T(4,128)} %param.8) | data formatting | bytes 96000 | tf_op args[1]
  2.2 17.3 %shard_map.86 = (f32[5,5,5,160]{3,2,1,0:T(8,128)}, f32[1,128]{1,0:T(1,128)}) custom-call(f32[5,5,160]{2,1,0:T(8,128)} %den_h.1, f32[3,5,5,160]{3,2,1,0:T(8,128)} %copy.9.vel_h, f32[5,5,160]{2,1,0:T(8,128)} %pre_h.1, f32[1,1,32]{2,1,0:T(1,128)} %ble_h.1, bf16[4,160,1024]{2,1,0:T(8,128)(2,1)} %wei_h.1, s32[1,120]{1,0:T(1,128)} %bitcast.3, s32[1,120]{1,0:T(1,128)} %bitcast.4), custom_call_target="tpu_custom_call" | custom-call | tf_op jit(solution)/shard_map/pallas_call | solution.py:412
  19.6 1.6 %copy.12 = f32[5,5,5,160]{3,2,1,0:T(8,128)} copy(f32[5,5,5,160]{3,2,1,0:T(8,128)} %get-tuple-element.8) | data formatting | bytes 160000
  21.2 1.1 %copy.13 = f32[128]{0:T(128)} copy(f32[128]{0:T(128)} %bitcast.5) | data formatting | bytes 1024
where the time goes:
time: 22.5 us; the launch traced here: 22.3 us
  Pallas kernels  17.3 us (77%)
  local copies, waits for them, and re-layouts  4.31 us (19%)
  between operations  0.64 us (3%)
    pallas_call x1, Pallas kernels, shards(): pl.pallas_call(functools.partial(kernel, sizes), out_shape=(jax.ShapeDtyp...  17.3 us
    unnamed x3, local copies, waits for them, and re-layouts  4.31 us

commit v1 on v0

--- a/solution.py
+++ b/solution.py
@@ -152,7 +152,7 @@
     for x in range(px):
         prim[0, x, 0:py, 0:pz] = den[x]
         for c in range(3):
-            prim[1 + c, x, 0:py, 0:pz] = vel[c, x]
+            prim[1 + c, x, 0:py, 0:pz] = vel[x, :, c, :]
         prim[4, x, 0:py, 0:pz] = pre[x]
 
     def mass_momentum(x, d):
@@ -399,6 +399,17 @@
     sig_ref[...] = total
 
 
+def write_out(tend_ref, sig_ref, tend_h, sig_h, sem):
+    copies = (
+        pltpu.make_async_copy(tend_ref, tend_h, sem.at[0]),
+        pltpu.make_async_copy(sig_ref, sig_h, sem.at[1]),
+    )
+    for copy in copies:
+        copy.start()
+    for copy in copies:
+        copy.wait()
+
+
 def shards(sizes, density, velocity, pressure, blending, face_signal_weights, surf_id, surface_face_code):
     groups = sizes[0] * sizes[1]
     px, py, pz = density.shape
@@ -411,15 +422,12 @@
     dma = pltpu.SemaphoreType.DMA
     tendency, signals = pl.pallas_call(
         functools.partial(kernel, sizes),
-        out_shape=(
-            jax.ShapeDtypeStruct((5, px, py, pz), F32),
-            jax.ShapeDtypeStruct((1, own), F32),
-        ),
+        out_shape=(pltpu.VMEM((5, px, py, pz), F32), pltpu.VMEM((1, own), F32)),
         in_specs=[pl.BlockSpec(memory_space=pl.ANY)] * 7,
         out_specs=(pl.BlockSpec(memory_space=pltpu.VMEM), pl.BlockSpec(memory_space=pltpu.VMEM)),
         scratch_shapes=[
             pltpu.VMEM(density.shape, F32),
-            pltpu.VMEM(velocity.shape, F32),
+            pltpu.VMEM((px, py, 3, pz), F32),
             pltpu.VMEM(pressure.shape, F32),
             pltpu.VMEM(blending.shape, F32),
             pltpu.VMEM(face_signal_weights.shape, BF16),
@@ -450,9 +458,21 @@
         ],
         compiler_params=pltpu.CompilerParams(collective_id=0, has_side_effects=True),
     )(
-        density, velocity, pressure, blending, face_signal_weights,
+        density, jnp.transpose(velocity, (1, 2, 0, 3)), pressure, blending, face_signal_weights,
         surf_id.reshape(1, -1), surface_face_code.reshape(1, -1),
     )
+    tendency = pltpu.with_memory_space_constraint(tendency, pltpu.VMEM)
+    signals = pltpu.with_memory_space_constraint(signals, pltpu.VMEM)
+    tendency, signals = pl.pallas_call(
+        write_out,
+        out_shape=(
+            jax.ShapeDtypeStruct((5, px, py, pz), F32),
+            jax.ShapeDtypeStruct((1, own), F32),
+        ),
+        in_specs=[pl.BlockSpec(memory_space=pltpu.VMEM)] * 2,
+        out_specs=(pl.BlockSpec(memory_space=pl.ANY), pl.BlockSpec(memory_space=pl.ANY)),
+        scratch_shapes=[dma((2,))],
+    )(tendency, signals)
     return tendency, signals.reshape(-1)
 
 

time: 22.5 us -> 18.2 us (0.81)
  local copies, waits for them, and re-layouts: 4.31 us -> 0 us
    unnamed x3 -> x0, local copies, waits for them, and re-layouts: 4.31 us -> none
    pallas_call x1 -> x2, Pallas kernels: 17.3 us -> 17.4 us  [the longest x1 16.7 us: shards(): pl.pallas_call(functools.partial(kernel, sizes), out_shape=(pltpu.VMEM((5...]
where the time goes in v1:
time: 18.2 us; the launch traced here: 18.1 us
  Pallas kernels  17.4 us (96%)
  between operations  0.64 us (4%)
    pallas_call x1, Pallas kernels, shards(): pl.pallas_call(functools.partial(kernel, sizes), out_shape=(pltpu.VMEM((5...  16.7 us
    pallas_call x1, Pallas kernels, shards(): pl.pallas_call(write_out, out_shape=(jax.ShapeDtypeStruct((5, px, py, pz)...  0.7 us

profile of v1, /device:TPU:0, one launch (start us, length us, event | category | flops | bytes accessed | tf_op | source)
XLA Modules:
  0.0 18.1 jit_solution(18041330128377236877)
XLA Ops:
  0.6 16.7 %shard_map.86 = (f32[5,5,5,160]{3,2,1,0:T(8,128)S(1)}, f32[1,128]{1,0:T(1,128)S(1)}) custom-call(f32[5,5,160]{2,1,0:T(8,128)} %den_h.1, f32[5,5,3,160]{3,2,1,0:T(4,128)} %bitcast.4, f32[5,5,160]{2,1,0:T(8,128)} %pre_h.1, f32[1,1,32]{2,1,0:T(1,128)} %ble_h.1, bf16[4,160,1024]{2,1,0:T(8,128)(2,1)} %wei_h.1, s32[1,120]{1,0:T(1,128)} %bitcast.5, s32[1,120]{1,0:T(1,128)} %bitcast.6), custom_call_target="tpu_custom_call" | custom-call | tf_op jit(solution)/shard_map/pallas_call | solution.py:423
  17.4 0.7 %shard_map.87 = (f32[5,5,5,160]{3,2,1,0:T(8,128)}, f32[1,128]{1,0:T(1,128)}) custom-call(f32[5,5,5,160]{3,2,1,0:T(8,128)S(1)} %get-tuple-element.6.tend_ref, f32[1,128]{1,0:T(1,128)S(1)} %get-tuple-element.7.sig_ref), custom_call_target="tpu_custom_call" | custom-call | tf_op jit(solution)/shard_map/pallas_call | solution.py:466

commit v2 on v1

--- a/solution.py
+++ b/solution.py
@@ -186,7 +186,7 @@
 
     for n in range(3, 6):
         loads[n].wait()
-    pad = mine.shape[-1]
+    pad = up(slots, 128)
     code_row = jnp.concatenate([codes[...], jnp.full((1, pad - slots), -1, jnp.int32)], axis=1) if pad > slots else codes[...]
     id_row = jnp.concatenate([ids[...], jnp.full((1, pad - slots), -1, jnp.int32)], axis=1) if pad > slots else ids[...]
     r_at = lax.broadcasted_iota(jnp.int32, (width, pad), 0)
@@ -201,8 +201,13 @@
         jnp.concatenate(chosen, axis=0),
         preferred_element_type=F32,
     )
-    slot_row = lax.broadcasted_iota(jnp.int32, (rows, pad), 0)
-    mine[...] = jnp.where(slot_row == quantities, id_row.astype(F32), face_values)
+    face_values = face_values.astype(BF16)
+    wanted = lax.broadcasted_iota(jnp.int32, (shard_faces, pad), 0)
+    for t in range(groups):
+        placing = jnp.where(id_row == wanted + t * shard_faces, F32(1), F32(0)).astype(BF16)
+        mine[t] = lax.dot_general(
+            face_values, placing, (((1,), (1,)), ((), ())), preferred_element_type=F32
+        ).astype(BF16)
 
     ystage[...] = jnp.ones(ystage.shape, F32)
     for x in range(px):
@@ -225,7 +230,10 @@
         )
 
     face_copies = [
-        remote(mine, faces_in.at[k - 1], face_send.at[k - 1], face_recv.at[k - 1], in_group(k))
+        remote(
+            mine.at[lax.rem(group + k, groups)], faces_in.at[k - 1],
+            face_send.at[k - 1], face_recv.at[k - 1], in_group(k),
+        )
         for k in range(1, groups)
     ]
     for copy in face_copies:
@@ -296,18 +304,10 @@
 
     for copy in face_copies:
         copy.wait()
-    wanted = lax.broadcasted_iota(jnp.int32, (shard_faces, pad), 0).astype(F32)
-    start = (group * shard_faces).astype(F32)
-    arrived = [mine[...]] + [faces_in[k] for k in range(groups - 1)]
-    placing = [
-        jnp.where(a[quantities : quantities + 1] - start == wanted, F32(1), F32(0)).astype(BF16) for a in arrived
-    ]
-    part[...] = lax.dot_general(
-        jnp.concatenate([a.astype(BF16) for a in arrived], axis=1),
-        jnp.concatenate(placing, axis=1),
-        (((1,), (1,)), ((), ())),
-        preferred_element_type=F32,
-    )
+    summed = mine[group].astype(F32)
+    for k in range(groups - 1):
+        summed = summed + faces_in[k].astype(F32)
+    part[...] = summed.astype(BF16)
     z_copies = [
         remote(part, parts_in.at[k - 1], z_send.at[k - 1], z_recv.at[k - 1], in_column(k))
         for k in range(1, nz_dev)
@@ -352,27 +352,12 @@
 
     lax.fori_loop(0, px, between, 0, unroll=True)
 
-    before = node_state(plane(px + 1), 0)
-    current = node_state(plane(0), 0)
-    below = rusanov2(before, current)
-    for x in range(px):
-        following = node_state(plane(x + 1), 0)
-        above = rusanov2(current, following)
-        half = F32(0.5 / QUAD[x])
-        for q in range(5):
-            out = acc[q, x]
-            mix = coef[21] * half
-            out = out - (half if x == px - 1 else mix) * above[q]
-            out = out + (half if x == 0 else mix) * below[q]
-            tend_ref[q, x] = out[0:py, 0:pz]
-        current, below = following, above
-
     for copy in z_copies:
         copy.wait()
     loads[6].wait()
-    data = part[...]
+    data = part[...].astype(F32)
     for k in range(nz_dev - 1):
-        data = data + parts_in[k]
+        data = data + parts_in[k].astype(F32)
     data = data.astype(BF16)
     data_row = lax.broadcasted_iota(jnp.int32, data.shape, 0)
     result = jnp.zeros((rows, local_signals), F32)
@@ -391,6 +376,21 @@
         )
     for copy in rs_copies:
         copy.start()
+    before = node_state(plane(px + 1), 0)
+    current = node_state(plane(0), 0)
+    below = rusanov2(before, current)
+    for x in range(px):
+        following = node_state(plane(x + 1), 0)
+        above = rusanov2(current, following)
+        half = F32(0.5 / QUAD[x])
+        for q in range(5):
+            out = acc[q, x]
+            mix = coef[21] * half
+            out = out - (half if x == px - 1 else mix) * above[q]
+            out = out + (half if x == 0 else mix) * below[q]
+            tend_ref[q, x] = out[0:py, 0:pz]
+        current, below = following, above
+
     for copy in rs_copies:
         copy.wait()
     total = stage[group]
@@ -416,7 +416,6 @@
     assert blending.shape[:2] == (1, 1) and px == NODES and py == NODES
     rows, lanes = up(py + 2, 8), up(pz + 2, 128)
     slots = surf_id.shape[0]
-    pad = up(slots, 128)
     quantities, shard_faces, local_signals = face_signal_weights.shape
     own = local_signals // groups
     dma = pltpu.SemaphoreType.DMA
@@ -440,10 +439,10 @@
             pltpu.VMEM((2, 5, rows, lanes), F32),
             pltpu.VMEM((2, rows, 128), F32),
             pltpu.VMEM((2, rows, 128), F32),
-            pltpu.VMEM((rows, pad), F32),
-            pltpu.VMEM((groups - 1, rows, pad), F32),
-            pltpu.VMEM((rows, shard_faces), F32),
-            pltpu.VMEM((sizes[2] - 1, rows, shard_faces), F32),
+            pltpu.VMEM((groups, rows, shard_faces), BF16),
+            pltpu.VMEM((groups - 1, rows, shard_faces), BF16),
+            pltpu.VMEM((rows, shard_faces), BF16),
+            pltpu.VMEM((sizes[2] - 1, rows, shard_faces), BF16),
             pltpu.VMEM((groups, 1, own), F32),
             pltpu.VMEM((groups - 1, 1, own), F32),
             dma((7,)),

time: 18.2 us -> 17.8 us (0.978)
  Pallas kernels: 17.4 us -> 17 us
    pallas_call x1, Pallas kernels: 16.7 us -> 16.3 us  [shards(): pl.pallas_call(functools.partial(kernel, sizes), out_shape=(pltpu.VMEM((5...]
where the time goes in v2:
time: 17.8 us; the launch traced here: 17.6 us
  Pallas kernels  17 us (96%)
  between operations  0.64 us (4%)
    pallas_call x1, Pallas kernels, shards(): pl.pallas_call(functools.partial(kernel, sizes), out_shape=(pltpu.VMEM((5...  16.3 us
    pallas_call x1, Pallas kernels, shards(): pl.pallas_call(write_out, out_shape=(jax.ShapeDtypeStruct((5, px, py, pz)...  0.7 us

profile of v2, /device:TPU:0, one launch (start us, length us, event | category | flops | bytes accessed | tf_op | source)
XLA Modules:
  0.0 17.6 jit_solution(11619139006740571166)
XLA Ops:
  0.6 16.3 %shard_map.86 = (f32[5,5,5,160]{3,2,1,0:T(8,128)S(1)}, f32[1,128]{1,0:T(1,128)S(1)}) custom-call(f32[5,5,160]{2,1,0:T(8,128)} %den_h.1, f32[5,5,3,160]{3,2,1,0:T(4,128)} %bitcast.4, f32[5,5,160]{2,1,0:T(8,128)} %pre_h.1, f32[1,1,32]{2,1,0:T(1,128)} %ble_h.1, bf16[4,160,1024]{2,1,0:T(8,128)(2,1)} %wei_h.1, s32[1,120]{1,0:T(1,128)} %bitcast.5, s32[1,120]{1,0:T(1,128)} %bitcast.6), custom_call_target="tpu_custom_call" | custom-call | tf_op jit(solution)/shard_map/pallas_call | solution.py:422
  16.9 0.7 %shard_map.87 = (f32[5,5,5,160]{3,2,1,0:T(8,128)}, f32[1,128]{1,0:T(1,128)}) custom-call(f32[5,5,5,160]{3,2,1,0:T(8,128)S(1)} %get-tuple-element.6.tend_ref, f32[1,128]{1,0:T(1,128)S(1)} %get-tuple-element.7.sig_ref), custom_call_target="tpu_custom_call" | custom-call | tf_op jit(solution)/shard_map/pallas_call | solution.py:465
